TPU v7x, 32 devices: a whole 2x2x4 slice. The times are simulated.
32 devices in a mesh: lat: 8 (over y, x, core), lon: 4 (over z).
Axes of the slice: x: 2, y: 2, z: 4, core: 2. Of those that a mesh axis runs over, the one named last changes fastest.
Arguments:
- right_side: float32 [256, 4096], P('lat', 'lon'), may hold values from -6 to 6
- coefficients: float32 [4, 256, 4096], P(None, 'lat', 'lon'), may hold values from 0.2 to 1.2
- extra: float32 [256, 4096], P('lat', 'lon'), may hold values from 0.05 to 1
- land_mask: int32 [256, 4096], P('lat', 'lon'), may hold values 0 or 1
Outputs:
- solution_field: float32 [256, 4096], P('lat', 'lon')
- residual: float32 [256, 4096], P('lat', 'lon')
- norms: float32 [3], replicated
All inputs are finite; a program needn't handle non-finite values. No bound on the sum of `land_mask` on one device may be relied on, other than what follows from the above.
Results may differ from a plain program's by a relative error of at most 0.00028.
Values sent between devices are 32-bit elements; how exact they have to be, the bound alone decides.
A program may use at most 64 MiB of HBM per device.

v0:
```python
import functools

import jax
import jax.numpy as jnp
from jax import lax
from jax.experimental import pallas as pl
from jax.experimental.pallas import tpu as pltpu
from jax.sharding import PartitionSpec as P

DEG = 4
ITERS = 3
LOW_EIG = 0.25
HIGH_EIG = 20.5
SHIFT = 0.8
LANES = 128
HALO = 16
VMEM_GRANT = 24 * 1024 * 1024
STRIP = 16
FIELDS = 7
PAIRS = (FIELDS + 1) // 2
MESH = pl.DeviceIdType.MESH
DIRS = [(a, b) for a in (-1, 0, 1) for b in (-1, 0, 1) if (a, b) != (0, 0)]


def level_factors():
    theta = (HIGH_EIG + LOW_EIG) / 2.0
    delta = (HIGH_EIG - LOW_EIG) / 2.0
    sigma = theta / delta
    rho = 1.0 / sigma
    out = []
    for _ in range(DEG - 1):
        rho_new = 1.0 / (2.0 * sigma - rho)
        out.append((rho_new * rho, 2.0 * rho_new / delta))
        rho = rho_new
    return theta, out


def scalars(h, g):
    c = SHIFT
    ht = [h[k + 1] + c * h[k] for k in range(len(h) - 1)]

    def form(a, t):
        total = None
        for k in range(2 * len(a) - 1):
            pairs = None
            for i in range(len(a)):
                j = k - i
                if 0 <= j < len(a) and i <= j:
                    term = a[i] * a[j]
                    if i != j:
                        term = term + term
                    pairs = term if pairs is None else pairs + term
            pairs = pairs * t[k]
            total = pairs if total is None else total + pairs
        return total

    one = jnp.ones_like(h[0])
    zero = jnp.zeros_like(h[0])
    a = [one]
    b = [one]
    gamma = h[0]
    norms = [g[0]]
    alpha = gamma / ht[0]
    x = [zero] * ITERS
    beta = zero
    for k in range(ITERS):
        if k > 0:
            b = [a[i] + (beta * b[i] if i < len(b) else 0.0) for i in range(len(a))]
        for i in range(len(b)):
            x[i] = x[i] + alpha * b[i]
        tb = [
            (b[i - 1] if i > 0 else zero) + (c * b[i] if i < len(b) else zero)
            for i in range(len(b) + 1)
        ]
        a = [(a[i] if i < len(a) else zero) - alpha * tb[i] for i in range(len(tb))]
        if k < ITERS - 1:
            gamma_new = form(a, h)
            dlt = form(a, ht)
            norms.append(form(a, g))
            beta = gamma_new / gamma
            alpha = gamma_new / (dlt - beta * gamma_new / alpha)
            gamma = gamma_new
    return x, a, norms


def kernel(
    nlat, nlon, rhs_in, coef_in, extra_in, mask_in, V, U, T_out,
    B, C, E, M, K, VC, UC, S, Z, SP, RP, SR, RR, G, GL, GZ, T2,
    loc_sem, snd, rcv, lat_s, lat_r, lon_s, lon_r,
):
    rows, cols = rhs_in.shape
    R = rows + 2 * HALO
    W = cols + 2 * LANES
    NC = W // LANES
    ilat = lax.axis_index("lat")
    ilon = lax.axis_index("lon")

    def cs_of(j):
        return slice(j * LANES, (j + 1) * LANES)

    mid = (pl.ds(HALO, rows), pl.ds(LANES, cols))
    local = [
        pltpu.make_async_copy(coef_in, C.at[:, mid[0], mid[1]], loc_sem.at[0]),
        pltpu.make_async_copy(mask_in, M.at[mid[0], mid[1]], loc_sem.at[1]),
        pltpu.make_async_copy(extra_in, E.at[mid[0], mid[1]], loc_sem.at[2]),
        pltpu.make_async_copy(rhs_in, B.at[mid[0], mid[1]], loc_sem.at[3]),
    ]
    for cp in local:
        cp.start()

    def lat_at(d):
        return lax.rem(ilat + d + nlat, nlat)

    def lon_at(d):
        return lax.rem(ilon + d + nlon, nlon)

    barrier = pltpu.get_barrier_semaphore()
    count = 0
    for d in range(1, nlat):
        pl.semaphore_signal(barrier, inc=1, device_id={"lat": lat_at(d)}, device_id_type=MESH)
        count += 1
    for d in range(1, nlon):
        pl.semaphore_signal(barrier, inc=1, device_id={"lon": lon_at(d)}, device_id_type=MESH)
        count += 1
    for a, b in DIRS:
        if a and b:
            pl.semaphore_signal(
                barrier, inc=1, device_id={"lat": lat_at(a), "lon": lon_at(b)}, device_id_type=MESH
            )
            count += 1

    def field(f, rws, cls):
        if f < 4:
            return C[f, rws, cls]
        if f == 4:
            return E[rws, cls]
        if f == 5:
            return B[rws, cls]
        return M[rws, cls].astype(jnp.float32)

    def put(f, rws, cls, value):
        if f < 4:
            C[f, rws, cls] = value
        elif f == 4:
            E[rws, cls] = value
        elif f == 5:
            B[rws, cls] = value
        else:
            M[rws, cls] = value.astype(jnp.int32)

    pl.semaphore_wait(barrier, count)

    sends = []

    def send(src, dst, a, b):
        i = len(sends)
        where = {}
        if a:
            where["lat"] = lat_at(a)
        if b:
            where["lon"] = lon_at(b)
        cp = pltpu.make_async_remote_copy(
            src_ref=src, dst_ref=dst, send_sem=snd.at[i], recv_sem=rcv.at[i],
            device_id=where, device_id_type=MESH,
        )
        cp.start()
        sends.append(cp)

    wide = pl.ds(LANES, cols)
    spans = {
        -1: (pl.ds(HALO, 8), pl.ds(HALO + rows, 8)),
        1: (pl.ds(HALO + rows - 8, 8), pl.ds(HALO - 8, 8)),
    }
    for ref, cp in zip((C, M, E, B), local):
        cp.wait()
        for a, (src, dst) in spans.items():
            if ref is C:
                send(C.at[:, src, wide], C.at[:, dst, wide], a, 0)
            else:
                send(ref.at[src, wide], ref.at[dst, wide], a, 0)

    own_rows = slice(HALO, HALO + rows)
    slot = lax.broadcasted_iota(jnp.int32, (rows, LANES), 1) // STRIP
    for side, chunk in ((0, 1), (1, NC - 2)):
        strip = jnp.zeros((rows, LANES), jnp.float32)
        for f in range(FIELDS):
            turn = (STRIP * f + side * STRIP) % LANES
            a = field(f, own_rows, cs_of(chunk))
            a = pltpu.roll(a, turn, 1) if turn else a
            strip = jnp.where(slot == f, a, strip)
        SP[side] = strip
    upper = lax.broadcasted_iota(jnp.int32, (8, cols), 0) >= 4
    inner = slice(LANES, LANES + cols)
    near = (slice(HALO + 8, HALO + 16), slice(HALO + rows - 16, HALO + rows - 8))
    for side in (0, 1):
        for t in range(PAIRS):
            a = field(2 * t, near[side], inner)
            if 2 * t + 1 < FIELDS:
                b = pltpu.roll(field(2 * t + 1, near[side], inner), 4, 0)
                a = jnp.where(upper, a, b) if side else jnp.where(upper, b, a)
            SR[side, t] = a
    for b in (-1, 1):
        side = (b + 1) // 2
        send(SP.at[side], RP.at[side, pl.ds(HALO, rows)], 0, b)
        for a in (-1, 1):
            src = pl.ds(0, HALO) if a < 0 else pl.ds(rows - HALO, HALO)
            dst = pl.ds(HALO + rows, HALO) if a < 0 else pl.ds(0, HALO)
            send(SP.at[side, src], RP.at[side, dst], a, b)
    for a in (-1, 1):
        side = (a + 1) // 2
        send(SR.at[side], RR.at[side], a, 0)
    for cp in sends:
        cp.wait_recv()

    every = slice(0, R)
    for side, chunk in ((0, NC - 1), (1, 0)):
        strip = RP[side]
        for f in range(FIELDS):
            turn = (-STRIP * f - side * STRIP) % LANES
            put(f, every, cs_of(chunk), pltpu.roll(strip, turn, 1) if turn else strip)
    far = (slice(R - 8, R), slice(0, 8))
    for side in (0, 1):
        for f in range(FIELDS):
            a = RR[side, f // 2]
            put(f, far[side], inner, pltpu.roll(a, 4, 0) if f % 2 else a)

    def shifts(read, n):
        lane = lax.broadcasted_iota(jnp.int32, (n, LANES), 1)
        first = lane == 0
        last = lane == LANES - 1
        memo = {}

        def get(kind, j):
            j = j % NC
            if (kind, j) not in memo:
                if kind == 0:
                    memo[kind, j] = read(j)
                else:
                    memo[kind, j] = pltpu.roll(get(0, j), 1 if kind < 0 else LANES - 1, 1)
            return memo[kind, j]

        def east(j):
            return jnp.where(last, get(1, j + 1), get(1, j))

        def west(j):
            return jnp.where(first, get(-1, j - 1), get(-1, j))

        return (lambda j: get(0, j)), east, west

    def north(a):
        return pltpu.roll(a, a.shape[0] - 1, 0)

    def south(a):
        return pltpu.roll(a, 1, 0)

    grow = lax.broadcasted_iota(jnp.int32, (R, LANES), 0) + (ilat * rows - HALO)
    keep = jnp.where((grow == nlat * rows - 1) | (grow == -1), 0.0, 1.0).astype(jnp.float32)

    mc, mE, mW = shifts(lambda j: M[:, cs_of(j)].astype(jnp.float32), R)
    for j in range(NC):
        m = mc(j)
        me = mE(j)
        mw = mW(j)
        mk = m * keep
        K[1][:, cs_of(j)] = C[0, :, cs_of(j)] * m * me
        K[6][:, cs_of(j)] = C[1, :, cs_of(j)] * mk * north(m)
        K[9][:, cs_of(j)] = C[2, :, cs_of(j)] * mk * north(me)
        K[10][:, cs_of(j)] = C[3, :, cs_of(j)] * mk * north(mw)
        VC[:, cs_of(j)] = B[:, cs_of(j)] * m

    cle, _, wle_of = shifts(lambda j: K[1][:, cs_of(j)], R)
    clne, _, wlne_of = shifts(lambda j: K[9][:, cs_of(j)], R)
    clnw, elnw_of, _ = shifts(lambda j: K[10][:, cs_of(j)], R)
    for j in range(NC):
        le = cle(j)
        wle = wle_of(j)
        ln = K[6][:, cs_of(j)]
        sln = south(ln)
        lne = clne(j)
        wlne = wlne_of(j)
        lnw = clnw(j)
        elnw = elnw_of(j)
        K[2][:, cs_of(j)] = wle
        K[3][:, cs_of(j)] = sln
        K[4][:, cs_of(j)] = south(lne)
        K[5][:, cs_of(j)] = south(lnw)
        K[7][:, cs_of(j)] = wlne
        K[8][:, cs_of(j)] = elnw
        d = E[:, cs_of(j)] + le + wle + ln + sln
        K[0][:, cs_of(j)] = d + lne + south(wlne) + lnw + south(elnw)

    theta, factors = level_factors()

    def apply(ref, rws, finish):
        n = rws.stop - rws.start
        centre, east, west = shifts(lambda j: ref[rws, cs_of(j)], n)
        for j in range(NC):
            v = centre(j)
            ve = east(j)
            vw = west(j)

            def k(i):
                return K[i][rws, cs_of(j)]

            p = k(3) * v + k(4) * ve + k(5) * vw
            q = k(6) * v + k(7) * vw + k(8) * ve
            finish(cs_of(j), v, k(0) * v - k(1) * ve - k(2) * vw - north(p) - south(q))

    mine = slice(HALO, HALO + rows)

    def round_of(it, rws):
        lo = HALO - rws.start

        def level0(cls, v, av):
            z = v * (1.0 / theta)
            step = factors[0][0] * z + factors[0][1] * (v - av * (1.0 / theta))
            S[rws, cls] = step
            Z[0][rws, cls] = z + step

        apply(VC, rws, level0)
        for level in range(1, DEG - 1):
            src = (level - 1) % 2

            def inner_level(cls, z, az):
                qq = VC[rws, cls] - az
                step = factors[level][0] * S[rws, cls] + factors[level][1] * qq
                new = z + step
                if level < DEG - 2:
                    S[rws, cls] = step
                    Z[1 - src][rws, cls] = new
                else:
                    UC[rws, cls] = new
                    U[it, :, cls] = new[lo : lo + rows]

            apply(Z[src], rws, inner_level)

        def last_level(cls, u, au):
            new = au - SHIFT * VC[rws, cls]
            VC[rws, cls] = new
            V[it + 1, :, cls] = new[lo : lo + rows]

        apply(UC, rws, last_level)

    for j in range(1, NC - 1):
        V[0, :, cs_of(j)] = VC[mine, cs_of(j)]
    round_of(0, slice(0, R))

    @pl.loop(1, ITERS)
    def _(it):
        round_of(it, slice(8, R - 8))

    hpairs = [((k + 1) // 2, k // 2) for k in range(2 * ITERS)]
    gpairs = [(k // 2, (k + 1) // 2) for k in range(2 * ITERS - 1)]

    def own(ref, n, j):
        return ref[n, :, cs_of(j)]

    def fold(a):
        return jnp.sum(a.reshape(rows // 8, 8, LANES), axis=0)

    def add(j, acc):
        v = [own(V, n, j) for n in range(ITERS + 1)]
        u = [own(U, n, j) for n in range(ITERS)]
        new = [fold(v[a] * u[b]) for a, b in hpairs] + [fold(v[a] * v[b]) for a, b in gpairs]
        return tuple(p + q for p, q in zip(acc, new))

    nsum = len(hpairs) + len(gpairs)
    acc = tuple(jnp.zeros((8, LANES), jnp.float32) for _ in range(nsum))
    for j in range(1, NC - 1):
        acc = add(j, acc)
    T2[...] = jnp.zeros_like(T2)
    for n, a in enumerate(acc):
        T2[n : n + 1, :] = jnp.sum(a, axis=0, keepdims=True)
    lo = T2[0:8, :]
    hi = T2[8:16, :]
    lo = lo + pltpu.roll(lo, LANES // 2, 1)
    hi = hi + pltpu.roll(hi, LANES // 2, 1)
    half = lax.broadcasted_iota(jnp.int32, (8, LANES), 1) < LANES // 2
    part = jnp.where(half, lo, hi)

    def exchange(part, slot, buf, axis, count, me, at, ssem, rsem):
        G[slot] = part
        buf[me] = part
        cps = []
        for d in range(1, count):
            cp = pltpu.make_async_remote_copy(
                src_ref=G.at[slot],
                dst_ref=buf.at[me],
                send_sem=ssem.at[d],
                recv_sem=rsem.at[d],
                device_id={axis: at(d)},
                device_id_type=MESH,
            )
            cp.start()
            cps.append(cp)
        for cp in cps:
            cp.wait_recv()
        total = buf[0]
        for n in range(1, count):
            total = total + buf[n]
        return total, cps

    total, c1 = exchange(part, 0, GL, "lat", nlat, ilat, lat_at, lat_s, lat_r)
    total, c2 = exchange(total, 1, GZ, "lon", nlon, ilon, lon_at, lon_s, lon_r)

    T_out[...] = total
    for cp in sends + c1 + c2:
        cp.wait_send()


def finish(V, U, T, x_out, r_out, n_out, XB, RB, T2, sems):
    total = T[...]
    rows, cols = XB.shape
    half = lax.broadcasted_iota(jnp.int32, (8, LANES), 1) < LANES // 2
    nh, ng = 2 * ITERS, 2 * ITERS - 1
    nsum = nh + ng
    for n, t in enumerate((jnp.where(half, total, 0.0), jnp.where(half, 0.0, total))):
        s = jnp.sum(t, axis=1, keepdims=True)
        T2[8 * n : 8 * n + 8, :] = jnp.broadcast_to(s, (8, LANES))
    sums = [T2[n : n + 1, :] for n in range(nsum)]
    xs, rs, norms = scalars(sums[:nh], sums[nh:])
    def cs_of(j):
        return slice(j * LANES, (j + 1) * LANES)
    cps = []
    for buf, out, co, src in ((XB, x_out, xs, U), (RB, r_out, rs, V)):
        for j in range(cols // LANES):
            x = co[0] * src[0, :, cs_of(j + 1)]
            for n in range(1, len(co)):
                x = x + co[n] * src[n, :, cs_of(j + 1)]
            buf[:, cs_of(j)] = x
        cp = pltpu.make_async_copy(buf, out, sems.at[len(cps)])
        cp.start()
        cps.append(cp)
    for n in range(ITERS):
        n_out[n] = norms[n][0, 0]
    for cp in cps:
        cp.wait()


def solution(mesh):
    nlat = mesh.shape["lat"]
    nlon = mesh.shape["lon"]

    def body(right_side, coefficients, extra, land_mask):
        rows, cols = right_side.shape
        R, W = rows + 2 * HALO, cols + 2 * LANES
        f32 = jnp.float32
        right_side, coefficients, extra, land_mask = (pltpu.with_memory_space_constraint(x, pltpu.HBM) for x in (right_side, coefficients, extra, land_mask))
        V, U, T = pl.pallas_call(
            functools.partial(kernel, nlat, nlon),
            out_shape=(
                pltpu.VMEM((ITERS + 1, rows, W), f32),
                pltpu.VMEM((ITERS, rows, W), f32),
                pltpu.VMEM((8, LANES), f32),
            ),
            in_specs=[pl.BlockSpec(memory_space=pl.ANY)] * 4,
            out_specs=(
                pl.BlockSpec(memory_space=pltpu.VMEM),
                pl.BlockSpec(memory_space=pltpu.VMEM),
                pl.BlockSpec(memory_space=pltpu.VMEM),
            ),
            scratch_shapes=[
                pltpu.VMEM((R, W), f32),
                pltpu.VMEM((4, R, W), f32),
                pltpu.VMEM((R, W), f32),
                pltpu.VMEM((R, W), jnp.int32),
                [pltpu.VMEM((R, W), f32)] * 11,
                pltpu.VMEM((R, W), f32),
                pltpu.VMEM((R, W), f32),
                pltpu.VMEM((R, W), f32),
                [pltpu.VMEM((R, W), f32)] * 2,
                pltpu.VMEM((2, rows, LANES), f32),
                pltpu.VMEM((2, R, LANES), f32),
                pltpu.VMEM((2, PAIRS, 8, cols), f32),
                pltpu.VMEM((2, PAIRS, 8, cols), f32),
                pltpu.VMEM((2, 8, LANES), f32),
                pltpu.VMEM((nlat, 8, LANES), f32),
                pltpu.VMEM((nlon, 8, LANES), f32),
                pltpu.VMEM((16, LANES), f32),
                pltpu.SemaphoreType.DMA((4,)),
                pltpu.SemaphoreType.DMA((16,)),
                pltpu.SemaphoreType.DMA((16,)),
                pltpu.SemaphoreType.DMA((nlat,)),
                pltpu.SemaphoreType.DMA((nlat,)),
                pltpu.SemaphoreType.DMA((nlon,)),
                pltpu.SemaphoreType.DMA((nlon,)),
            ],
            compiler_params=pltpu.CompilerParams(
                collective_id=0, has_side_effects=True, vmem_limit_bytes=VMEM_GRANT
            ),
        )(right_side, coefficients, extra, land_mask)
        return pl.pallas_call(
            finish,
            out_shape=(
                jax.ShapeDtypeStruct((rows, cols), f32),
                jax.ShapeDtypeStruct((rows, cols), f32),
                jax.ShapeDtypeStruct((ITERS,), f32),
            ),
            in_specs=[pl.BlockSpec(memory_space=pltpu.VMEM)] * 3,
            out_specs=(
                pl.BlockSpec(memory_space=pl.ANY),
                pl.BlockSpec(memory_space=pl.ANY),
                pl.BlockSpec(memory_space=pltpu.SMEM),
            ),
            scratch_shapes=[
                pltpu.VMEM((rows, cols), f32),
                pltpu.VMEM((rows, cols), f32),
                pltpu.VMEM((16, LANES), f32),
                pltpu.SemaphoreType.DMA((2,)),
            ],
            compiler_params=pltpu.CompilerParams(vmem_limit_bytes=4 * 1024 * 1024),
        )(V, U, T)

    return jax.shard_map(
        body,
        mesh=mesh,
        in_specs=(P("lat", "lon"), P(None, "lat", "lon"), P("lat", "lon"), P("lat", "lon")),
        out_specs=(P("lat", "lon"), P("lat", "lon"), P()),
        check_vma=False,
    )
```

profile of v0, /device:TPU:0, one launch (start us, length us, event | category | flops | bytes accessed | tf_op | source)
XLA Modules:
  0.0 29.6 jit_solution(6264647738621093739)
XLA Ops:
  0.6 27.6 %shard_map.67 = (f32[4,32,1280]{2,1,0:T(8,128)S(1)}, f32[3,32,1280]{2,1,0:T(8,128)S(1)}, f32[8,128]{1,0:T(8,128)S(1)}) custom-call(f32[32,1024]{1,0:T(8,128)} %rhs_in.1, f32[4,32,1024]{2,1,0:T(8,128)} %coef_in.1, f32[32,1024]{1,0:T(8,128)} %extra_in.1, s32[32,1024]{1,0:T(8,128)} %mask_in.1), custom_call_target="tpu_custom_call" | custom-call | tf_op jit(solution)/shard_map/pallas_call | solution.py:449
  28.2 1.4 %shard_map.68 = (f32[32,1024]{1,0:T(8,128)}, f32[32,1024]{1,0:T(8,128)}, f32[3]{0:T(128)}) custom-call(f32[4,32,1280]{2,1,0:T(8,128)S(1)} %get-tuple-element.6.V, f32[3,32,1280]{2,1,0:T(8,128)S(1)} %get-tuple-element.7.U, f32[8,128]{1,0:T(8,128)S(1)} %get-tuple-element.8.T), custom_call_target="tpu_custom_call" | custom-call | tf_op jit(solution)/shard_map/pallas_call | solution.py:492
where the time goes:
time: 29.7 us; the launch traced here: 29.6 us
  Pallas kernels  29 us (98%)
  between operations  0.64 us (2%)
    pallas_call x1, Pallas kernels, body(): pl.pallas_call(functools.partial(kernel, nlat, nlon), out_shape=(pltpu.VM...  27.6 us
    pallas_call x1, Pallas kernels, body(): pl.pallas_call(finish, out_shape=(jax.ShapeDtypeStruct((rows, cols), f32)...  1.4 us

commit v1 on v0

v1 whole, which is shorter than its diff:
```python
import functools

import jax
import jax.numpy as jnp
from jax import lax
from jax.experimental import pallas as pl
from jax.experimental.pallas import tpu as pltpu
from jax.sharding import PartitionSpec as P

DEG = 4
ITERS = 3
LOW_EIG = 0.25
HIGH_EIG = 20.5
SHIFT = 0.8
LANES = 128
TILE = 8
HALF = 4
STRIP = 16
FIELDS = 7
NGROUPS = 2
ALL_TO_ALL = 64
VMEM_GRANT = 24 * 1024 * 1024
FINISH_GRANT = 4 * 1024 * 1024
MESH = pl.DeviceIdType.MESH


def level_factors():
    theta = (HIGH_EIG + LOW_EIG) / 2.0
    delta = (HIGH_EIG - LOW_EIG) / 2.0
    sigma = theta / delta
    rho = 1.0 / sigma
    out = []
    for _ in range(DEG - 1):
        rho_new = 1.0 / (2.0 * sigma - rho)
        out.append((rho_new * rho, 2.0 * rho_new / delta))
        rho = rho_new
    return theta, out


def scalars(h, g):
    c = SHIFT
    ht = [h[k + 1] + c * h[k] for k in range(len(h) - 1)]

    def form(a, t):
        total = None
        for k in range(2 * len(a) - 1):
            pairs = None
            for i in range(len(a)):
                j = k - i
                if 0 <= j < len(a) and i <= j:
                    term = a[i] * a[j]
                    if i != j:
                        term = term + term
                    pairs = term if pairs is None else pairs + term
            pairs = pairs * t[k]
            total = pairs if total is None else total + pairs
        return total

    one = jnp.ones_like(h[0])
    zero = jnp.zeros_like(h[0])
    a = [one]
    b = [one]
    gamma = h[0]
    norms = [g[0]]
    alpha = gamma / ht[0]
    x = [zero] * ITERS
    beta = zero
    for k in range(ITERS):
        if k > 0:
            b = [a[i] + (beta * b[i] if i < len(b) else 0.0) for i in range(len(a))]
        for i in range(len(b)):
            x[i] = x[i] + alpha * b[i]
        tb = [
            (b[i - 1] if i > 0 else zero) + (c * b[i] if i < len(b) else zero)
            for i in range(len(b) + 1)
        ]
        a = [(a[i] if i < len(a) else zero) - alpha * tb[i] for i in range(len(tb))]
        if k < ITERS - 1:
            gamma_new = form(a, h)
            dlt = form(a, ht)
            norms.append(form(a, g))
            beta = gamma_new / gamma
            alpha = gamma_new / (dlt - beta * gamma_new / alpha)
            gamma = gamma_new
    return x, a, norms


HPAIRS = [((k + 1) // 2, k // 2) for k in range(2 * ITERS)]
GPAIRS = [(k // 2, (k + 1) // 2) for k in range(2 * ITERS - 1)]
NSUM = len(HPAIRS) + len(GPAIRS)


def cs_of(j):
    return slice(j * LANES, (j + 1) * LANES)


def ts_of(i):
    return slice(i * TILE, (i + 1) * TILE)


def groups_of(nc, count):
    if count == 1:
        return [(0, nc)], [list(range(nc + 1))]
    edges = [-(-nc * g // count) for g in range(count + 1)]
    spans = [(edges[g], edges[g + 1]) for g in range(count)]
    lists = []
    for g, (lo, hi) in enumerate(spans):
        own = list(range(lo, hi))
        own = [nc] + own if g == 0 else [lo - 1] + own
        lists.append(own + [nc] if g == count - 1 else own)
    return spans, lists


def kernel(
    nlat, nlon, rhs_in, coef_in, extra_in, mask_in, V, U, T_out,
    C, E, B, M, HC, HE, HB, HM, SR, RR, SP, RP, CP, K, L2, VC, S, Z, GS, G, G2,
    loc_sem, snd, rcv, red_s, red_r, ready,
):
    rows, cols = rhs_in.shape
    nr = rows // TILE
    nc = cols // LANES
    depth = ITERS
    ilat = lax.axis_index("lat")
    ilon = lax.axis_index("lon")
    has_n = ilat < nlat - 1
    has_s = ilat > 0

    local = [
        pltpu.make_async_copy(coef_in, C, loc_sem.at[0]),
        pltpu.make_async_copy(mask_in, M, loc_sem.at[1]),
        pltpu.make_async_copy(extra_in, E, loc_sem.at[2]),
        pltpu.make_async_copy(rhs_in, B, loc_sem.at[3]),
    ]
    for cp in local:
        cp.start()

    def lat_at(d):
        return lax.rem(ilat + d + nlat, nlat)

    def lon_at(d):
        return lax.rem(ilon + d + nlon, nlon)

    def where_to(a, b):
        out = {}
        if a:
            out["lat"] = lat_at(a)
        if b:
            out["lon"] = lon_at(b)
        return out

    barrier = pltpu.get_barrier_semaphore()

    def greet(sem, a, b):
        pl.semaphore_signal(sem, inc=1, device_id=where_to(a, b), device_id_type=MESH)

    for d in range(1, nlat):
        greet(barrier, d, 0)
    for d in range(1, nlon):
        greet(barrier, 0, d)
    for a, there in ((-1, has_s), (1, has_n)):

        @pl.when(there)
        def _():
            greet(barrier, a, -1)
            greet(barrier, a, 1)

    for side, there in ((0, has_n), (1, has_s)):

        @pl.when(jnp.logical_not(there))
        def _():
            for ref in (HC, HE, HB, HM, RR):
                ref[side] = jnp.zeros(ref.shape[1:], ref.dtype)
            for e in (0, 1):
                CP[e, side] = jnp.zeros(CP.shape[2:], jnp.float32)

    for cp in local:
        cp.wait()

    def own_field(f, rws, cls):
        if f < 4:
            return C[f, rws, cls]
        if f == 4:
            return E[rws, cls]
        if f == 5:
            return B[rws, cls]
        return M[rws, cls].astype(jnp.float32)

    sub = lax.broadcasted_iota(jnp.int32, (TILE, LANES), 0)
    lane = lax.broadcasted_iota(jnp.int32, (TILE, LANES), 1)
    slot = lane // STRIP
    for side, chunk in ((0, 0), (1, nc - 1)):
        for i in range(nr):
            strip = jnp.zeros((TILE, LANES), jnp.float32)
            for f in range(FIELDS):
                turn = (STRIP * f + side * STRIP) % LANES
                a = own_field(f, ts_of(i), cs_of(chunk))
                a = pltpu.roll(a, turn, 1) if turn else a
                strip = jnp.where(slot == f, a, strip)
            SP[side, ts_of(i), :] = strip
    far = (slice(TILE, TILE + HALF), slice(rows - TILE - HALF, rows - TILE))
    for side in (0, 1):
        for f in range(FIELDS):
            SR[side, f] = own_field(f, far[side], slice(0, cols))

    count = nlat - 1 + nlon - 1 + 2 * (has_n.astype(jnp.int32) + has_s.astype(jnp.int32))
    pl.semaphore_wait(barrier, count)
    direct = nlat * nlon <= ALL_TO_ALL
    if direct:
        for d in range(1, nlon):
            greet(ready, 0, d)

    sends = []

    def send(src, dst, a, b, stage):
        i = len(sends)
        cp = pltpu.make_async_remote_copy(
            src_ref=src, dst_ref=dst, send_sem=snd.at[i], recv_sem=rcv.at[i],
            device_id=where_to(a, b), device_id_type=MESH,
        )
        sends.append((cp, a, stage))
        return cp

    def each(cps, a, sending, act):
        def run():
            for cp in cps:
                act(cp)

        if a == 0:
            run()
        elif cps:
            pl.when((has_s if a < 0 else has_n) if sending else (has_n if a < 0 else has_s))(run)

    def start(cps, a):
        each(cps, a, True, lambda cp: cp.start())

    spans, lists = groups_of(nc, NGROUPS)
    start([send(SP.at[(b + 1) // 2], RP.at[(b + 1) // 2], 0, b, 0) for b in (-1, 1)], 0)
    for a in (-1, 1):
        side = (a + 1) // 2
        src = pl.ds(0, STRIP) if a < 0 else pl.ds(rows - STRIP, STRIP)
        start([send(SP.at[e, src], CP.at[e, side], a, 2 * e - 1, 0) for e in (0, 1)], a)
    for g, (lo, hi) in enumerate(spans):
        cl = pl.ds(lo * LANES, (hi - lo) * LANES)
        for a in (-1, 1):
            side = (a + 1) // 2
            edge = pl.ds(0, TILE) if a < 0 else pl.ds(rows - TILE, TILE)
            cps = [send(C.at[:, edge, cl], HC.at[side, :, :, cl], a, 0, g)]
            cps.append(send(M.at[edge, cl], HM.at[side, :, cl], a, 0, g))
            cps.append(send(E.at[edge, cl], HE.at[side, :, cl], a, 0, g))
            cps.append(send(B.at[edge, cl], HB.at[side, :, cl], a, 0, g))
            cps.append(send(SR.at[side, :, :, cl], RR.at[side, :, :, cl], a, 0, g))
            start(cps, a)

    up = sub < HALF
    s0 = sub == 0
    s3 = sub == HALF - 1
    s4 = sub == HALF
    s7 = sub == TILE - 1
    first = lane == 0
    last = lane == LANES - 1
    rim = (lane < STRIP) | (lane >= LANES - STRIP)

    def roll0(a, n):
        return pltpu.roll(a, n, 0)

    def halo_field(f, side, cls):
        if f < 4:
            return HC[side, f, :, cls]
        if f == 4:
            return HE[side, :, cls]
        if f == 5:
            return HB[side, :, cls]
        return HM[side, :, cls].astype(jnp.float32)

    def onion(n8, s8):
        near = jnp.where(up, n8, s8)
        return [near, jnp.where(up, roll0(n8, HALF), roll0(s8, HALF))]

    def raw(f, j):
        if j < nc:
            tiles = [own_field(f, ts_of(i), cs_of(j)) for i in range(nr)]
            tiles += onion(halo_field(f, 0, cs_of(j)), halo_field(f, 1, cs_of(j)))
            outer = [RR[side, f, :, cs_of(j)] for side in (0, 1)]
            return tiles + [jnp.concatenate(outer, axis=0)]

        def turned(read):
            out = []
            for e in (0, 1):
                turn = (-STRIP * f - e * STRIP) % LANES
                a = read(e)
                out.append(pltpu.roll(a, turn, 1) if turn else a)
            return jnp.where(lane < LANES // 2, out[0], out[1])

        tiles = [turned(lambda e, i=i: RP[e, ts_of(i), :]) for i in range(nr)]
        n8, n16 = (turned(lambda e, i=i: CP[e, 0, ts_of(i), :]) for i in (0, 1))
        s16, s8 = (turned(lambda e, i=i: CP[e, 1, ts_of(i), :]) for i in (0, 1))
        tiles = tiles + onion(n8, s8) + [jnp.where(up, n16, s16)]
        return [jnp.where(rim, t, 0.0) for t in tiles] if f == 6 else tiles

    def north(t, n):
        memo = {}

        def r3(i):
            if i not in memo:
                memo[i] = roll0(t[i], HALF - 1)
            return memo[i]

        r7 = [roll0(a, TILE - 1) for a in t]
        out = []
        for i in range(n):
            if i < nr:
                out.append(jnp.where(s7, r7[i + 1], r7[i]))
                continue
            a = jnp.where(s7, r7[0] if i == nr else r3(i - 1), r7[i])
            out.append(jnp.where(s3, r3(i + 1), a) if i + 1 < len(t) else a)
        return out

    def south(t, n):
        memo = {}

        def r5(i):
            if i not in memo:
                memo[i] = roll0(t[i], HALF + 1)
            return memo[i]

        r1 = [roll0(a, 1) for a in t]
        out = []
        for i in range(n):
            if i < nr:
                out.append(jnp.where(s0, r1[i - 1] if i else r1[nr], r1[i]))
                continue
            a = jnp.where(s0, r1[nr - 1] if i == nr else r5(i - 1), r1[i])
            out.append(jnp.where(s4, r5(i + 1), a) if i + 1 < len(t) else a)
        return out

    def shifts(read, order, ring):
        memo = {}

        def get(kind, p):
            p = p % len(order)
            if (kind, p) not in memo:
                if kind == 0:
                    memo[kind, p] = read(order[p])
                else:
                    turn = 1 if kind < 0 else LANES - 1
                    memo[kind, p] = [pltpu.roll(a, turn, 1) for a in get(0, p)]
            return memo[kind, p]

        def east(p):
            if p + 1 == len(order) and not ring:
                return get(1, p)
            return [jnp.where(last, b, a) for a, b in zip(get(1, p), get(1, p + 1))]

        def west(p):
            if p == 0 and not ring:
                return get(-1, p)
            return [jnp.where(first, b, a) for a, b in zip(get(-1, p), get(-1, p - 1))]

        return (lambda p: get(0, p)), east, west

    full = nr + depth

    def put(ref, k, j, tiles):
        for i, t in enumerate(tiles):
            ref[k, ts_of(i), cs_of(j)] = t

    def links(order, ring):
        mc, me_of, mw_of = shifts(lambda j: raw(6, j), order, ring)
        for p, j in enumerate(order):
            m, me, mw = mc(p), me_of(p), mw_of(p)
            nm, nme, nmw = north(m, full), north(me, full), north(mw, full)
            for k, f, o in ((1, 0, me), (6, 1, nm)):
                put(K, k, j, [c * a * b for c, a, b in zip(raw(f, j), m, o)])
            for k, f, o in ((0, 2, nme), (1, 3, nmw)):
                put(L2, k, j, [c * a * b for c, a, b in zip(raw(f, j), m, o)])
            for i, (a, b) in enumerate(zip(m, raw(5, j))):
                VC[ts_of(i), cs_of(j)] = a * b

        def tiles_of(ref, k):
            return lambda j: [ref[k, ts_of(i), cs_of(j)] for i in range(full)]

        cle, _, wle_of = shifts(tiles_of(K, 1), order, ring)
        clne, _, wlne_of = shifts(tiles_of(L2, 0), order, ring)
        clnw, elnw_of, _ = shifts(tiles_of(L2, 1), order, ring)
        for p, j in enumerate(order):
            le, wle, lne, wlne = cle(p), wle_of(p), clne(p), wlne_of(p)
            lnw, elnw = clnw(p), elnw_of(p)
            ln = tiles_of(K, 6)(j)
            sln = south(ln, full)
            swlne, selnw = south(wlne, full), south(elnw, full)
            put(K, 2, j, wle)
            put(K, 3, j, sln)
            put(K, 4, j, south(lne, full))
            put(K, 5, j, south(lnw, full))
            put(K, 7, j, wlne)
            put(K, 8, j, elnw)
            for i, d in enumerate(raw(4, j)):
                d = d + le[i] + wle[i] + ln[i] + sln[i]
                K[0, ts_of(i), cs_of(j)] = d + lne[i] + swlne[i] + lnw[i] + selnw[i]

    def apply(order, ring, ref, n_in, n_out, finish):
        centre, east, west = shifts(
            lambda j: [ref[ts_of(i), cs_of(j)] for i in range(n_in)], order, ring
        )
        used = min(n_in, n_out + 1)
        for p, j in enumerate(order):
            v, ve, vw = centre(p), east(p), west(p)

            def k(n, i):
                return K[n, ts_of(i), cs_of(j)]

            up_part = [k(3, i) * v[i] + k(4, i) * ve[i] + k(5, i) * vw[i] for i in range(used)]
            low_part = [k(6, i) * v[i] + k(7, i) * vw[i] + k(8, i) * ve[i] for i in range(used)]
            np_ = north(up_part, n_out)
            sq = south(low_part, n_out)
            for i in range(n_out):
                a = k(0, i) * v[i] - k(1, i) * ve[i] - k(2, i) * vw[i] - np_[i] - sq[i]
                finish(i, j, v[i], a)

    theta, factors = level_factors()
    seen = set()

    def record(ref, n, i, j, value):
        if i >= nr or j == nc:
            return
        if j in seen:
            value = jnp.where(lane < LANES // 2, ref[n, ts_of(i), cs_of(j)], value)
        ref[n, ts_of(i), cs_of(j)] = value

    def rounds(order, ring):
        for j in order:
            for i in range(nr):
                record(V, 0, i, j, VC[ts_of(i), cs_of(j)])
        for it in range(ITERS):
            n = full - it

            def level0(i, j, v, av):
                z = v * (1.0 / theta)
                step = factors[0][0] * z + factors[0][1] * (v - av * (1.0 / theta))
                S[ts_of(i), cs_of(j)] = step
                Z[0, ts_of(i), cs_of(j)] = z + step

            apply(order, ring, VC, n, n, level0)
            for level in range(1, DEG - 1):
                src = (level - 1) % 2

                def inner_level(i, j, z, az):
                    at = (ts_of(i), cs_of(j))
                    step = factors[level][0] * S[at] + factors[level][1] * (VC[at] - az)
                    new = z + step
                    Z[1 - src, ts_of(i), cs_of(j)] = new
                    if level < DEG - 2:
                        S[at] = step
                    else:
                        record(U, it, i, j, new)

                apply(order, ring, Z.at[src], n, n, inner_level)

            def last_level(i, j, u, au):
                at = (ts_of(i), cs_of(j))
                new = au - SHIFT * VC[at]
                VC[at] = new
                record(V, it + 1, i, j, new)

            apply(order, ring, Z.at[(DEG - 2) % 2], n, n - 1, last_level)

    acc = [None] * NSUM
    waited = 0
    for g, order in enumerate(lists):
        for a in (0, -1, 1):
            cps = [cp for cp, d, stage in sends if d == a and stage == g]
            each(cps, a, False, lambda cp: cp.wait_recv())
        ring = len(lists) == 1
        links(order, ring)
        rounds(order, ring)
        done = [j for j in order if j < nc and (ring or g == len(lists) - 1 or j != order[-1])]
        for j in done:
            for i in range(nr):
                v = [V[n, ts_of(i), cs_of(j)] for n in range(ITERS + 1)]
                u = [U[n, ts_of(i), cs_of(j)] for n in range(ITERS)]
                new = [v[a] * u[b] for a, b in HPAIRS] + [v[a] * v[b] for a, b in GPAIRS]
                acc = [b if a is None else a + b for a, b in zip(acc, new)]
        seen.update(j for j in order if j < nc)

    row = jnp.zeros((TILE, LANES), jnp.float32)
    for n, a in enumerate(acc):
        row = jnp.where(lane == n, jnp.sum(a, axis=1, keepdims=True), row)
    row = jnp.sum(row, axis=0, keepdims=True)

    pending = []

    def gather(row, stage, buf, me, peers):
        GS[stage] = row
        buf[me] = row
        cps = []
        for a, b in peers:
            i = len(pending)
            cp = pltpu.make_async_remote_copy(
                src_ref=GS.at[stage], dst_ref=buf.at[me],
                send_sem=red_s.at[i], recv_sem=red_r.at[i],
                device_id=where_to(a, b), device_id_type=MESH,
            )
            cp.start()
            cps.append(cp)
            pending.append(cp)
        for cp in cps:
            cp.wait_recv()
        parts = [buf[n] for n in range(buf.shape[0])]
        while len(parts) > 1:
            odd = parts[len(parts) // 2 * 2 :]
            parts = [a + b for a, b in zip(parts[::2], parts[1::2])] + odd
        return parts[0]

    if direct:
        pl.semaphore_wait(ready, nlon - 1)
        peers = [(a, b) for a in range(nlat) for b in range(nlon) if a or b]
        row = gather(row, 0, G, ilat * nlon + ilon, peers)
    else:
        row = gather(row, 0, G, ilat, [(d, 0) for d in range(1, nlat)])
        row = gather(row, 1, G2, ilon, [(0, d) for d in range(1, nlon)])
    T_out[...] = jnp.broadcast_to(row, (TILE, LANES))

    for a in (0, -1, 1):
        cps = [cp for cp, d, _ in sends if d == a]
        each(cps, a, True, lambda cp: cp.wait_send())
    for cp in pending:
        cp.wait_send()


def finish(V, U, T, x_out, r_out, n_out, X, R, sems):
    rows, cols = X.shape
    total = T[...]
    sums = [jnp.broadcast_to(total[:, n : n + 1], (TILE, LANES)) for n in range(NSUM)]
    xs, rs, norms = scalars(sums[: len(HPAIRS)], sums[len(HPAIRS) :])
    cps = []
    for buf, out, co, src in ((X, x_out, xs, U), (R, r_out, rs, V)):
        for j in range(cols // LANES):
            for i in range(rows // TILE):
                at = (ts_of(i), cs_of(j))
                a = co[0] * src[0, ts_of(i), cs_of(j)]
                for n in range(1, len(co)):
                    a = a + co[n] * src[n, ts_of(i), cs_of(j)]
                buf[at] = a
        cp = pltpu.make_async_copy(buf, out, sems.at[len(cps)])
        cp.start()
        cps.append(cp)
    for n in range(ITERS):
        n_out[n] = norms[n][0, 0]
    for cp in cps:
        cp.wait()


def solution(mesh):
    nlat = mesh.shape["lat"]
    nlon = mesh.shape["lon"]

    def body(*args):
        rows, cols = args[0].shape
        nc = cols // LANES
        W = cols + LANES
        R = rows + ITERS * TILE
        f32, i32 = jnp.float32, jnp.int32
        ndev = nlat * nlon
        direct = ndev <= ALL_TO_ALL
        npeers = ndev - 1 if direct else nlat + nlon - 2
        nsend = 6 + 10 * NGROUPS
        vmem, dma = pltpu.VMEM, pltpu.SemaphoreType.DMA
        args = [pltpu.with_memory_space_constraint(a, pltpu.HBM) for a in args]
        V, U, T = pl.pallas_call(
            functools.partial(kernel, nlat, nlon),
            out_shape=(
                vmem((ITERS + 1, rows, cols), f32),
                vmem((ITERS, rows, cols), f32),
                vmem((TILE, LANES), f32),
            ),
            in_specs=[pl.BlockSpec(memory_space=pl.ANY)] * 4,
            out_specs=(pl.BlockSpec(memory_space=pltpu.VMEM),) * 3,
            scratch_shapes=[
                vmem((4, rows, cols), f32),
                vmem((rows, cols), f32),
                vmem((rows, cols), f32),
                vmem((rows, cols), i32),
                vmem((2, 4, TILE, cols), f32),
                vmem((2, TILE, cols), f32),
                vmem((2, TILE, cols), f32),
                vmem((2, TILE, cols), i32),
                vmem((2, FIELDS, HALF, cols), f32),
                vmem((2, FIELDS, HALF, cols), f32),
                vmem((2, rows, LANES), f32),
                vmem((2, rows, LANES), f32),
                vmem((2, 2, STRIP, LANES), f32),
                vmem((9, R, W), f32),
                vmem((2, R, W), f32),
                vmem((R, W), f32),
                vmem((R, W), f32),
                vmem((2, R, W), f32),
                vmem((2, 1, LANES), f32),
                vmem((ndev if direct else nlat, 1, LANES), f32),
                vmem((nlon, 1, LANES), f32),
                dma((4,)),
                dma((nsend,)),
                dma((nsend,)),
                dma((npeers,)),
                dma((npeers,)),
                pltpu.SemaphoreType.REGULAR,
            ],
            compiler_params=pltpu.CompilerParams(
                collective_id=0, has_side_effects=True, vmem_limit_bytes=VMEM_GRANT
            ),
        )(*args)
        return pl.pallas_call(
            finish,
            out_shape=(
                jax.ShapeDtypeStruct((rows, cols), f32),
                jax.ShapeDtypeStruct((rows, cols), f32),
                jax.ShapeDtypeStruct((ITERS,), f32),
            ),
            in_specs=[pl.BlockSpec(memory_space=pltpu.VMEM)] * 3,
            out_specs=(
                pl.BlockSpec(memory_space=pl.ANY),
                pl.BlockSpec(memory_space=pl.ANY),
                pl.BlockSpec(memory_space=pltpu.SMEM),
            ),
            scratch_shapes=[vmem((rows, cols), f32), vmem((rows, cols), f32), dma((2,))],
            compiler_params=pltpu.CompilerParams(vmem_limit_bytes=FINISH_GRANT),
        )(V, U, T)

    return jax.shard_map(
        body,
        mesh=mesh,
        in_specs=(P("lat", "lon"), P(None, "lat", "lon"), P("lat", "lon"), P("lat", "lon")),
        out_specs=(P("lat", "lon"), P("lat", "lon"), P()),
        check_vma=False,
    )
```

time: 29.7 us -> 25.2 us (0.85)
  Pallas kernels: 29 us -> 24.4 us
    pallas_call x1, Pallas kernels: 27.6 us -> 23 us  [body(): pl.pallas_call(functools.partial(kernel, nlat, nlon), out_shape=(vmem((IT...]
where the time goes in v1:
time: 25.2 us; the launch traced here: 25 us
  Pallas kernels  24.4 us (97%)
  between operations  0.64 us (3%)
    pallas_call x1, Pallas kernels, body(): pl.pallas_call(functools.partial(kernel, nlat, nlon), out_shape=(vmem((IT...  23 us
    pallas_call x1, Pallas kernels, body(): pl.pallas_call(finish, out_shape=(jax.ShapeDtypeStruct((rows, cols), f32)...  1.39 us

profile of v1, /device:TPU:0, one launch (start us, length us, event | category | flops | bytes accessed | tf_op | source)
XLA Modules:
  0.0 25.0 jit_solution(16732252302707085461)
XLA Ops:
  0.6 23.0 %shard_map.67 = (f32[4,32,1024]{2,1,0:T(8,128)S(1)}, f32[3,32,1024]{2,1,0:T(8,128)S(1)}, f32[8,128]{1,0:T(8,128)S(1)}) custom-call(f32[32,1024]{1,0:T(8,128)} %rhs_in.1, f32[4,32,1024]{2,1,0:T(8,128)} %coef_in.1, f32[32,1024]{1,0:T(8,128)} %extra_in.1, s32[32,1024]{1,0:T(8,128)} %mask_in.1), custom_call_target="tpu_custom_call" | custom-call | tf_op jit(solution)/shard_map/pallas_call | solution.py:569
  23.6 1.4 %shard_map.68 = (f32[32,1024]{1,0:T(8,128)}, f32[32,1024]{1,0:T(8,128)}, f32[3]{0:T(128)}) custom-call(f32[4,32,1024]{2,1,0:T(8,128)S(1)} %get-tuple-element.6.V, f32[3,32,1024]{2,1,0:T(8,128)S(1)} %get-tuple-element.7.U, f32[8,128]{1,0:T(8,128)S(1)} %get-tuple-element.8.T), custom_call_target="tpu_custom_call" | custom-call | tf_op jit(solution)/shard_map/pallas_call | solution.py:611

commit v2 on v1

--- a/solution.py
+++ b/solution.py
@@ -24,17 +24,19 @@
 MESH = pl.DeviceIdType.MESH
 
 
-def level_factors():
+def factored():
     theta = (HIGH_EIG + LOW_EIG) / 2.0
     delta = (HIGH_EIG - LOW_EIG) / 2.0
     sigma = theta / delta
     rho = 1.0 / sigma
-    out = []
+    step = at_zero = 1.0 / theta
     for _ in range(DEG - 1):
         rho_new = 1.0 / (2.0 * sigma - rho)
-        out.append((rho_new * rho, 2.0 * rho_new / delta))
+        step = rho_new * rho * step + 2.0 * rho_new / delta
+        at_zero = at_zero + step
         rho = rho_new
-    return theta, out
+    bump = theta * theta - delta * delta
+    return theta, bump, at_zero / (-2.0 * theta * (theta * theta + bump))
 
 
 def scalars(h, g):
@@ -113,8 +115,8 @@
 
 def kernel(
     nlat, nlon, rhs_in, coef_in, extra_in, mask_in, V, U, T_out,
-    C, E, B, M, HC, HE, HB, HM, SR, RR, SP, RP, CP, K, L2, VC, S, Z, GS, G, G2,
-    loc_sem, snd, rcv, red_s, red_r, ready,
+    C, E, B, M, HC, HE, HB, HM, SR, RR, SP, RP, CP, K, L2, VC, Z, GS, G, G2,
+    LC, LE, LB, LM, LR, loc_sem, snd, rcv, red_s, red_r, rel_s, rel_r, ready,
 ):
     rows, cols = rhs_in.shape
     nr = rows // TILE
@@ -185,23 +187,6 @@
             return B[rws, cls]
         return M[rws, cls].astype(jnp.float32)
 
-    sub = lax.broadcasted_iota(jnp.int32, (TILE, LANES), 0)
-    lane = lax.broadcasted_iota(jnp.int32, (TILE, LANES), 1)
-    slot = lane // STRIP
-    for side, chunk in ((0, 0), (1, nc - 1)):
-        for i in range(nr):
-            strip = jnp.zeros((TILE, LANES), jnp.float32)
-            for f in range(FIELDS):
-                turn = (STRIP * f + side * STRIP) % LANES
-                a = own_field(f, ts_of(i), cs_of(chunk))
-                a = pltpu.roll(a, turn, 1) if turn else a
-                strip = jnp.where(slot == f, a, strip)
-            SP[side, ts_of(i), :] = strip
-    far = (slice(TILE, TILE + HALF), slice(rows - TILE - HALF, rows - TILE))
-    for side in (0, 1):
-        for f in range(FIELDS):
-            SR[side, f] = own_field(f, far[side], slice(0, cols))
-
     count = nlat - 1 + nlon - 1 + 2 * (has_n.astype(jnp.int32) + has_s.astype(jnp.int32))
     pl.semaphore_wait(barrier, count)
     direct = nlat * nlon <= ALL_TO_ALL
@@ -209,7 +194,15 @@
         for d in range(1, nlon):
             greet(ready, 0, d)
 
+    sub = lax.broadcasted_iota(jnp.int32, (TILE, LANES), 0)
+    lane = lax.broadcasted_iota(jnp.int32, (TILE, LANES), 1)
+    slot = lane // STRIP
     sends = []
+    relays = []
+    mid = nlat // 2 - 1
+    relaying = nlat % 2 == 0 and nlat >= 4
+    at_mid = {1: ilat == mid, -1: ilat == mid + 1}
+    at_relay = {1: ilat == nlat - 1, -1: ilat == 0}
 
     def send(src, dst, a, b, stage):
         i = len(sends)
@@ -233,23 +226,99 @@
     def start(cps, a):
         each(cps, a, True, lambda cp: cp.start())
 
+    def detour(src, via, dst, a, i):
+        k = len(relays)
+        ends = {1: (nlat - 1, mid + 1), -1: (0, mid)}[a]
+        legs = [
+            pltpu.make_async_remote_copy(
+                src_ref=src, dst_ref=via, send_sem=snd.at[i], recv_sem=rel_r.at[k],
+                device_id={"lat": ends[0]}, device_id_type=MESH,
+            ),
+            pltpu.make_async_remote_copy(
+                src_ref=via, dst_ref=dst, send_sem=rel_s.at[k], recv_sem=rcv.at[i],
+                device_id={"lat": ends[1]}, device_id_type=MESH,
+            ),
+        ]
+        relays.append((legs, a))
+        return legs
+
     spans, lists = groups_of(nc, NGROUPS)
-    start([send(SP.at[(b + 1) // 2], RP.at[(b + 1) // 2], 0, b, 0) for b in (-1, 1)], 0)
-    for a in (-1, 1):
-        side = (a + 1) // 2
-        src = pl.ds(0, STRIP) if a < 0 else pl.ds(rows - STRIP, STRIP)
-        start([send(SP.at[e, src], CP.at[e, side], a, 2 * e - 1, 0) for e in (0, 1)], a)
+    ng = len(spans)
+    stage_of = (ng - 1, 0)
     for g, (lo, hi) in enumerate(spans):
         cl = pl.ds(lo * LANES, (hi - lo) * LANES)
+        relayed = relaying and g == ng - 1
+        batches = {}
         for a in (-1, 1):
             side = (a + 1) // 2
             edge = pl.ds(0, TILE) if a < 0 else pl.ds(rows - TILE, TILE)
-            cps = [send(C.at[:, edge, cl], HC.at[side, :, :, cl], a, 0, g)]
-            cps.append(send(M.at[edge, cl], HM.at[side, :, cl], a, 0, g))
-            cps.append(send(E.at[edge, cl], HE.at[side, :, cl], a, 0, g))
-            cps.append(send(B.at[edge, cl], HB.at[side, :, cl], a, 0, g))
-            cps.append(send(SR.at[side, :, :, cl], RR.at[side, :, :, cl], a, 0, g))
-            start(cps, a)
+            moves = [
+                (C.at[:, edge, cl], LC, HC.at[side, :, :, cl]),
+                (M.at[edge, cl], LM, HM.at[side, :, cl]),
+                (E.at[edge, cl], LE, HE.at[side, :, cl]),
+                (B.at[edge, cl], LB, HB.at[side, :, cl]),
+                (SR.at[side, :, :, cl], LR, RR.at[side, :, :, cl]),
+            ]
+            base = len(sends)
+            cps = [send(src, dst, a, 0, g) for src, _, dst in moves]
+            legs = [detour(*move, a, base + n) for n, move in enumerate(moves)] if relayed else []
+            batches[a] = (cps, legs)
+
+        def launch(a, part):
+            cps, legs = batches[a]
+            if not legs:
+                start(cps[part], a)
+                return
+            there = has_s if a < 0 else has_n
+
+            @pl.when(there & jnp.logical_not(at_mid[a]))
+            def _():
+                for cp in cps[part]:
+                    cp.start()
+
+            @pl.when(at_mid[a])
+            def _():
+                for leg, _ in legs[part]:
+                    leg.start()
+
+        if g == 0:
+            for a in (-1, 1):
+                launch(a, slice(0, 4))
+            for side, chunk in ((0, 0), (1, nc - 1)):
+                for i in range(nr):
+                    strip = jnp.zeros((TILE, LANES), jnp.float32)
+                    for f in range(FIELDS):
+                        turn = (STRIP * f + side * STRIP) % LANES
+                        a = own_field(f, ts_of(i), cs_of(chunk))
+                        a = pltpu.roll(a, turn, 1) if turn else a
+                        strip = jnp.where(slot == f, a, strip)
+                    SP[side, ts_of(i), :] = strip
+            start([send(SP.at[e], RP.at[e], 0, 2 * e - 1, stage_of[e]) for e in (1, 0)], 0)
+            far = (slice(TILE, TILE + HALF), slice(rows - TILE - HALF, rows - TILE))
+            for side in (0, 1):
+                for f in range(FIELDS):
+                    SR[side, f] = own_field(f, far[side], slice(0, cols))
+            for a in (-1, 1):
+                launch(a, slice(4, 5))
+        else:
+            for a in (-1, 1):
+                launch(a, slice(0, 5))
+        for e in (0, 1):
+            if stage_of[e] != g:
+                continue
+            for a in (-1, 1):
+                src = pl.ds(0, STRIP) if a < 0 else pl.ds(rows - STRIP, STRIP)
+                start([send(SP.at[e, src], CP.at[e, (a + 1) // 2], a, 2 * e - 1, g)], a)
+
+    for a in (-1, 1):
+        mine = [legs for legs, d in relays if d == a]
+        if mine:
+
+            @pl.when(at_relay[a])
+            def _():
+                for first, second in mine:
+                    first.wait_recv()
+                    second.start()
 
     up = sub < HALF
     s0 = sub == 0
@@ -258,7 +327,7 @@
     s7 = sub == TILE - 1
     first = lane == 0
     last = lane == LANES - 1
-    rim = (lane < STRIP) | (lane >= LANES - STRIP)
+    rims = (lane < STRIP, lane >= LANES - STRIP)
 
     def roll0(a, n):
         return pltpu.roll(a, n, 0)
@@ -276,7 +345,7 @@
         near = jnp.where(up, n8, s8)
         return [near, jnp.where(up, roll0(n8, HALF), roll0(s8, HALF))]
 
-    def raw(f, j):
+    def raw(f, j, ends):
         if j < nc:
             tiles = [own_field(f, ts_of(i), cs_of(j)) for i in range(nr)]
             tiles += onion(halo_field(f, 0, cs_of(j)), halo_field(f, 1, cs_of(j)))
@@ -285,17 +354,20 @@
 
         def turned(read):
             out = []
-            for e in (0, 1):
+            for e in ends:
                 turn = (-STRIP * f - e * STRIP) % LANES
                 a = read(e)
                 out.append(pltpu.roll(a, turn, 1) if turn else a)
-            return jnp.where(lane < LANES // 2, out[0], out[1])
+            return jnp.where(lane < LANES // 2, out[0], out[1]) if len(out) > 1 else out[0]
 
         tiles = [turned(lambda e, i=i: RP[e, ts_of(i), :]) for i in range(nr)]
         n8, n16 = (turned(lambda e, i=i: CP[e, 0, ts_of(i), :]) for i in (0, 1))
         s16, s8 = (turned(lambda e, i=i: CP[e, 1, ts_of(i), :]) for i in (0, 1))
         tiles = tiles + onion(n8, s8) + [jnp.where(up, n16, s16)]
-        return [jnp.where(rim, t, 0.0) for t in tiles] if f == 6 else tiles
+        if f < 6:
+            return tiles
+        rim = rims[ends[0]] if len(ends) == 1 else rims[0] | rims[1]
+        return [jnp.where(rim, t, 0.0) for t in tiles]
 
     def north(t, n):
         memo = {}
@@ -359,21 +431,22 @@
         return (lambda p: get(0, p)), east, west
 
     full = nr + depth
+    theta, bump, scale = factored()
 
     def put(ref, k, j, tiles):
         for i, t in enumerate(tiles):
             ref[k, ts_of(i), cs_of(j)] = t
 
-    def links(order, ring):
-        mc, me_of, mw_of = shifts(lambda j: raw(6, j), order, ring)
+    def links(order, ring, ends):
+        mc, me_of, mw_of = shifts(lambda j: raw(6, j, ends), order, ring)
         for p, j in enumerate(order):
             m, me, mw = mc(p), me_of(p), mw_of(p)
             nm, nme, nmw = north(m, full), north(me, full), north(mw, full)
             for k, f, o in ((1, 0, me), (6, 1, nm)):
-                put(K, k, j, [c * a * b for c, a, b in zip(raw(f, j), m, o)])
+                put(K, k, j, [c * a * b for c, a, b in zip(raw(f, j, ends), m, o)])
             for k, f, o in ((0, 2, nme), (1, 3, nmw)):
-                put(L2, k, j, [c * a * b for c, a, b in zip(raw(f, j), m, o)])
-            for i, (a, b) in enumerate(zip(m, raw(5, j))):
+                put(L2, k, j, [c * a * b for c, a, b in zip(raw(f, j, ends), m, o)])
+            for i, (a, b) in enumerate(zip(m, raw(5, j, ends))):
                 VC[ts_of(i), cs_of(j)] = a * b
 
         def tiles_of(ref, k):
@@ -394,16 +467,21 @@
             put(K, 5, j, south(lnw, full))
             put(K, 7, j, wlne)
             put(K, 8, j, elnw)
-            for i, d in enumerate(raw(4, j)):
+            for i, d in enumerate(raw(4, j, ends)):
                 d = d + le[i] + wle[i] + ln[i] + sln[i]
-                K[0, ts_of(i), cs_of(j)] = d + lne[i] + swlne[i] + lnw[i] + selnw[i]
-
-    def apply(order, ring, ref, n_in, n_out, finish):
+                d = d + lne[i] + swlne[i] + lnw[i] + selnw[i]
+                K[0, ts_of(i), cs_of(j)] = d
+                K[9, ts_of(i), cs_of(j)] = d - theta
+                K[10, ts_of(i), cs_of(j)] = d - 2.0 * theta
+
+    def apply(order, ring, ref, diag, n_in, n_out, finish, skip=()):
         centre, east, west = shifts(
             lambda j: [ref[ts_of(i), cs_of(j)] for i in range(n_in)], order, ring
         )
         used = min(n_in, n_out + 1)
         for p, j in enumerate(order):
+            if j in skip:
+                continue
             v, ve, vw = centre(p), east(p), west(p)
 
             def k(n, i):
@@ -414,10 +492,9 @@
             np_ = north(up_part, n_out)
             sq = south(low_part, n_out)
             for i in range(n_out):
-                a = k(0, i) * v[i] - k(1, i) * ve[i] - k(2, i) * vw[i] - np_[i] - sq[i]
-                finish(i, j, v[i], a)
-
-    theta, factors = level_factors()
+                a = k(diag, i) * v[i] - k(1, i) * ve[i] - k(2, i) * vw[i] - np_[i] - sq[i]
+                finish(i, j, a)
+
     seen = set()
 
     def record(ref, n, i, j, value):
@@ -434,35 +511,29 @@
         for it in range(ITERS):
             n = full - it
 
-            def level0(i, j, v, av):
-                z = v * (1.0 / theta)
-                step = factors[0][0] * z + factors[0][1] * (v - av * (1.0 / theta))
-                S[ts_of(i), cs_of(j)] = step
-                Z[0, ts_of(i), cs_of(j)] = z + step
-
-            apply(order, ring, VC, n, n, level0)
-            for level in range(1, DEG - 1):
-                src = (level - 1) % 2
-
-                def inner_level(i, j, z, az):
-                    at = (ts_of(i), cs_of(j))
-                    step = factors[level][0] * S[at] + factors[level][1] * (VC[at] - az)
-                    new = z + step
-                    Z[1 - src, ts_of(i), cs_of(j)] = new
-                    if level < DEG - 2:
-                        S[at] = step
-                    else:
-                        record(U, it, i, j, new)
-
-                apply(order, ring, Z.at[src], n, n, inner_level)
-
-            def last_level(i, j, u, au):
+            def level0(i, j, a):
+                Z[0, ts_of(i), cs_of(j)] = a
+
+            def level1(i, j, a):
                 at = (ts_of(i), cs_of(j))
-                new = au - SHIFT * VC[at]
-                VC[at] = new
+                Z[1, ts_of(i), cs_of(j)] = scale * a + (scale * bump) * VC[at]
+
+            def level2(i, j, a):
+                Z[0, ts_of(i), cs_of(j)] = a
+                record(U, it, i, j, a)
+
+            def last_level(i, j, a):
+                at = (ts_of(i), cs_of(j))
+                new = a - SHIFT * VC[at]
+                if it < ITERS - 1:
+                    VC[at] = new
                 record(V, it + 1, i, j, new)
 
-            apply(order, ring, Z.at[(DEG - 2) % 2], n, n - 1, last_level)
+            apply(order, ring, VC, 9, n, n, level0)
+            apply(order, ring, Z.at[0], 9, n, n, level1)
+            apply(order, ring, Z.at[1], 10, n, n, level2)
+            skip = (nc,) if it == ITERS - 1 else ()
+            apply(order, ring, Z.at[0], 0, n, n - 1, last_level, skip)
 
     acc = [None] * NSUM
     waited = 0
@@ -471,7 +542,7 @@
             cps = [cp for cp, d, stage in sends if d == a and stage == g]
             each(cps, a, False, lambda cp: cp.wait_recv())
         ring = len(lists) == 1
-        links(order, ring)
+        links(order, ring, [e for e in (0, 1) if stage_of[e] == g])
         rounds(order, ring)
         done = [j for j in order if j < nc and (ring or g == len(lists) - 1 or j != order[-1])]
         for j in done:
@@ -488,6 +559,30 @@
     row = jnp.sum(row, axis=0, keepdims=True)
 
     pending = []
+    paired = nlat & (nlat - 1) == 0
+
+    def peer(a, b):
+        if not paired:
+            return where_to(a, b)
+        to, bit = ilat, 1
+        while bit < nlat:
+            if a & bit:
+                to = to + bit - 2 * bit * (lax.div(ilat, bit) % 2)
+            bit *= 2
+        return {"lat": to, "lon": lon_at(b)}
+
+    def drain():
+        for a in (0, -1, 1):
+            cps = [cp for cp, d, _ in sends if d == a]
+            each(cps, a, True, lambda cp: cp.wait_send())
+        for a in (-1, 1):
+            mine = [legs for legs, d in relays if d == a]
+            if mine:
+
+                @pl.when(at_relay[a])
+                def _():
+                    for _, second in mine:
+                        second.wait_send()
 
     def gather(row, stage, buf, me, peers):
         GS[stage] = row
@@ -498,12 +593,16 @@
             cp = pltpu.make_async_remote_copy(
                 src_ref=GS.at[stage], dst_ref=buf.at[me],
                 send_sem=red_s.at[i], recv_sem=red_r.at[i],
-                device_id=where_to(a, b), device_id_type=MESH,
+                device_id=peer(a, b), device_id_type=MESH,
             )
             cp.start()
             cps.append(cp)
             pending.append(cp)
+        if stage == 0:
+            drain()
         for cp in cps:
+            cp.wait_send()
+        for cp in cps[::-1]:
             cp.wait_recv()
         parts = [buf[n] for n in range(buf.shape[0])]
         while len(parts) > 1:
@@ -513,18 +612,12 @@
 
     if direct:
         pl.semaphore_wait(ready, nlon - 1)
-        peers = [(a, b) for a in range(nlat) for b in range(nlon) if a or b]
+        peers = [(a, b) for a in range(nlat) for b in range(nlon) if a or b][::-1]
         row = gather(row, 0, G, ilat * nlon + ilon, peers)
     else:
         row = gather(row, 0, G, ilat, [(d, 0) for d in range(1, nlat)])
         row = gather(row, 1, G2, ilon, [(0, d) for d in range(1, nlon)])
     T_out[...] = jnp.broadcast_to(row, (TILE, LANES))
-
-    for a in (0, -1, 1):
-        cps = [cp for cp, d, _ in sends if d == a]
-        each(cps, a, True, lambda cp: cp.wait_send())
-    for cp in pending:
-        cp.wait_send()
 
 
 def finish(V, U, T, x_out, r_out, n_out, X, R, sems):
@@ -564,6 +657,8 @@
         direct = ndev <= ALL_TO_ALL
         npeers = ndev - 1 if direct else nlat + nlon - 2
         nsend = 6 + 10 * NGROUPS
+        lo, hi = groups_of(nc, NGROUPS)[0][-1]
+        half = (hi - lo) * LANES
         vmem, dma = pltpu.VMEM, pltpu.SemaphoreType.DMA
         args = [pltpu.with_memory_space_constraint(a, pltpu.HBM) for a in args]
         V, U, T = pl.pallas_call(
@@ -589,19 +684,25 @@
                 vmem((2, rows, LANES), f32),
                 vmem((2, rows, LANES), f32),
                 vmem((2, 2, STRIP, LANES), f32),
-                vmem((9, R, W), f32),
+                vmem((11, R, W), f32),
                 vmem((2, R, W), f32),
-                vmem((R, W), f32),
                 vmem((R, W), f32),
                 vmem((2, R, W), f32),
                 vmem((2, 1, LANES), f32),
                 vmem((ndev if direct else nlat, 1, LANES), f32),
                 vmem((nlon, 1, LANES), f32),
+                vmem((4, TILE, half), f32),
+                vmem((TILE, half), f32),
+                vmem((TILE, half), f32),
+                vmem((TILE, half), i32),
+                vmem((FIELDS, HALF, half), f32),
                 dma((4,)),
                 dma((nsend,)),
                 dma((nsend,)),
                 dma((npeers,)),
                 dma((npeers,)),
+                dma((10,)),
+                dma((10,)),
                 pltpu.SemaphoreType.REGULAR,
             ],
             compiler_params=pltpu.CompilerParams(

time: 25.2 us -> 23.2 us (0.921)
  Pallas kernels: 24.4 us -> 22.5 us
    pallas_call x1, Pallas kernels: 23 us -> 21.1 us  [body(): pl.pallas_call(functools.partial(kernel, nlat, nlon), out_shape=(vmem((IT...]
where the time goes in v2:
time: 23.2 us; the launch traced here: 23.1 us
  Pallas kernels  22.5 us (97%)
  between operations  0.64 us (3%)
    pallas_call x1, Pallas kernels, body(): pl.pallas_call(functools.partial(kernel, nlat, nlon), out_shape=(vmem((IT...  21.1 us
    pallas_call x1, Pallas kernels, body(): pl.pallas_call(finish, out_shape=(jax.ShapeDtypeStruct((rows, cols), f32)...  1.39 us

profile of v2, /device:TPU:0, one launch (start us, length us, event | category | flops | bytes accessed | tf_op | source)
XLA Modules:
  0.0 23.1 jit_solution(13258668875618809859)
XLA Ops:
  0.6 21.1 %shard_map.67 = (f32[4,32,1024]{2,1,0:T(8,128)S(1)}, f32[3,32,1024]{2,1,0:T(8,128)S(1)}, f32[8,128]{1,0:T(8,128)S(1)}) custom-call(f32[32,1024]{1,0:T(8,128)} %rhs_in.1, f32[4,32,1024]{2,1,0:T(8,128)} %coef_in.1, f32[32,1024]{1,0:T(8,128)} %extra_in.1, s32[32,1024]{1,0:T(8,128)} %mask_in.1), custom_call_target="tpu_custom_call" | custom-call | tf_op jit(solution)/shard_map/pallas_call | solution.py:664
  21.7 1.4 %shard_map.68 = (f32[32,1024]{1,0:T(8,128)}, f32[32,1024]{1,0:T(8,128)}, f32[3]{0:T(128)}) custom-call(f32[4,32,1024]{2,1,0:T(8,128)S(1)} %get-tuple-element.6.V, f32[3,32,1024]{2,1,0:T(8,128)S(1)} %get-tuple-element.7.U, f32[8,128]{1,0:T(8,128)S(1)} %get-tuple-element.8.T), custom_call_target="tpu_custom_call" | custom-call | tf_op jit(solution)/shard_map/pallas_call | solution.py:712

commit v3 on v2

--- a/solution.py
+++ b/solution.py
@@ -115,8 +115,8 @@
 
 def kernel(
     nlat, nlon, rhs_in, coef_in, extra_in, mask_in, V, U, T_out,
-    C, E, B, M, HC, HE, HB, HM, SR, RR, SP, RP, CP, K, L2, VC, Z, GS, G, G2,
-    LC, LE, LB, LM, LR, loc_sem, snd, rcv, red_s, red_r, rel_s, rel_r, ready,
+    C, E, B, M, SR, RR, SP, RP, CP, K, L2, VC, Z, GS, G, G2,
+    LR, loc_sem, snd, rcv, red_s, red_r, rel_s, rel_r, ready,
 ):
     rows, cols = rhs_in.shape
     nr = rows // TILE
@@ -170,8 +170,7 @@
 
         @pl.when(jnp.logical_not(there))
         def _():
-            for ref in (HC, HE, HB, HM, RR):
-                ref[side] = jnp.zeros(ref.shape[1:], ref.dtype)
+            RR[side] = jnp.zeros(RR.shape[1:], jnp.float32)
             for e in (0, 1):
                 CP[e, side] = jnp.zeros(CP.shape[2:], jnp.float32)
 
@@ -245,45 +244,31 @@
     spans, lists = groups_of(nc, NGROUPS)
     ng = len(spans)
     stage_of = (ng - 1, 0)
+
+    def half_rows(side, k):
+        first = k * HALF if side == 0 else rows - (k + 1) * HALF
+        return slice(first, first + HALF)
+
     for g, (lo, hi) in enumerate(spans):
+        for side in (0, 1):
+            for f in range(FIELDS):
+                for k in range(depth):
+                    for j in range(lo, hi):
+                        SR[side, f * depth + k, :, cs_of(j)] = own_field(f, half_rows(side, k), cs_of(j))
         cl = pl.ds(lo * LANES, (hi - lo) * LANES)
-        relayed = relaying and g == ng - 1
-        batches = {}
         for a in (-1, 1):
             side = (a + 1) // 2
-            edge = pl.ds(0, TILE) if a < 0 else pl.ds(rows - TILE, TILE)
-            moves = [
-                (C.at[:, edge, cl], LC, HC.at[side, :, :, cl]),
-                (M.at[edge, cl], LM, HM.at[side, :, cl]),
-                (E.at[edge, cl], LE, HE.at[side, :, cl]),
-                (B.at[edge, cl], LB, HB.at[side, :, cl]),
-                (SR.at[side, :, :, cl], LR, RR.at[side, :, :, cl]),
-            ]
-            base = len(sends)
-            cps = [send(src, dst, a, 0, g) for src, _, dst in moves]
-            legs = [detour(*move, a, base + n) for n, move in enumerate(moves)] if relayed else []
-            batches[a] = (cps, legs)
-
-        def launch(a, part):
-            cps, legs = batches[a]
-            if not legs:
-                start(cps[part], a)
-                return
+            move = (SR.at[side, :, :, cl], LR, RR.at[side, :, :, cl])
+            i = len(sends)
+            cp = send(move[0], move[2], a, 0, g)
+            if not (relaying and g == ng - 1):
+                start([cp], a)
+                continue
+            leg = detour(*move, a, i)[0]
             there = has_s if a < 0 else has_n
-
-            @pl.when(there & jnp.logical_not(at_mid[a]))
-            def _():
-                for cp in cps[part]:
-                    cp.start()
-
-            @pl.when(at_mid[a])
-            def _():
-                for leg, _ in legs[part]:
-                    leg.start()
-
+            pl.when(there & jnp.logical_not(at_mid[a]))(lambda: cp.start())
+            pl.when(at_mid[a])(lambda: leg.start())
         if g == 0:
-            for a in (-1, 1):
-                launch(a, slice(0, 4))
             for side, chunk in ((0, 0), (1, nc - 1)):
                 for i in range(nr):
                     strip = jnp.zeros((TILE, LANES), jnp.float32)
@@ -294,15 +279,6 @@
                         strip = jnp.where(slot == f, a, strip)
                     SP[side, ts_of(i), :] = strip
             start([send(SP.at[e], RP.at[e], 0, 2 * e - 1, stage_of[e]) for e in (1, 0)], 0)
-            far = (slice(TILE, TILE + HALF), slice(rows - TILE - HALF, rows - TILE))
-            for side in (0, 1):
-                for f in range(FIELDS):
-                    SR[side, f] = own_field(f, far[side], slice(0, cols))
-            for a in (-1, 1):
-                launch(a, slice(4, 5))
-        else:
-            for a in (-1, 1):
-                launch(a, slice(0, 5))
         for e in (0, 1):
             if stage_of[e] != g:
                 continue
@@ -332,15 +308,6 @@
     def roll0(a, n):
         return pltpu.roll(a, n, 0)
 
-    def halo_field(f, side, cls):
-        if f < 4:
-            return HC[side, f, :, cls]
-        if f == 4:
-            return HE[side, :, cls]
-        if f == 5:
-            return HB[side, :, cls]
-        return HM[side, :, cls].astype(jnp.float32)
-
     def onion(n8, s8):
         near = jnp.where(up, n8, s8)
         return [near, jnp.where(up, roll0(n8, HALF), roll0(s8, HALF))]
@@ -348,9 +315,10 @@
     def raw(f, j, ends):
         if j < nc:
             tiles = [own_field(f, ts_of(i), cs_of(j)) for i in range(nr)]
-            tiles += onion(halo_field(f, 0, cs_of(j)), halo_field(f, 1, cs_of(j)))
-            outer = [RR[side, f, :, cs_of(j)] for side in (0, 1)]
-            return tiles + [jnp.concatenate(outer, axis=0)]
+            for k in range(depth):
+                halves = [RR[side, f * depth + k, :, cs_of(j)] for side in (0, 1)]
+                tiles.append(jnp.concatenate(halves, axis=0))
+            return tiles
 
         def turned(read):
             out = []
@@ -620,12 +588,15 @@
     T_out[...] = jnp.broadcast_to(row, (TILE, LANES))
 
 
-def finish(V, U, T, x_out, r_out, n_out, X, R, sems):
+def finish(V, U, T, x_out, r_out, n_out, X, R, N, sems):
     rows, cols = X.shape
     total = T[...]
     sums = [jnp.broadcast_to(total[:, n : n + 1], (TILE, LANES)) for n in range(NSUM)]
     xs, rs, norms = scalars(sums[: len(HPAIRS)], sums[len(HPAIRS) :])
-    cps = []
+    for n in range(ITERS):
+        N[n] = norms[n][0, 0]
+    cps = [pltpu.make_async_copy(N, n_out, sems.at[0])]
+    cps[0].start()
     for buf, out, co, src in ((X, x_out, xs, U), (R, r_out, rs, V)):
         for j in range(cols // LANES):
             for i in range(rows // TILE):
@@ -637,8 +608,6 @@
         cp = pltpu.make_async_copy(buf, out, sems.at[len(cps)])
         cp.start()
         cps.append(cp)
-    for n in range(ITERS):
-        n_out[n] = norms[n][0, 0]
     for cp in cps:
         cp.wait()
 
@@ -656,7 +625,7 @@
         ndev = nlat * nlon
         direct = ndev <= ALL_TO_ALL
         npeers = ndev - 1 if direct else nlat + nlon - 2
-        nsend = 6 + 10 * NGROUPS
+        nsend = 6 + 2 * NGROUPS
         lo, hi = groups_of(nc, NGROUPS)[0][-1]
         half = (hi - lo) * LANES
         vmem, dma = pltpu.VMEM, pltpu.SemaphoreType.DMA
@@ -675,12 +644,8 @@
                 vmem((rows, cols), f32),
                 vmem((rows, cols), f32),
                 vmem((rows, cols), i32),
-                vmem((2, 4, TILE, cols), f32),
-                vmem((2, TILE, cols), f32),
-                vmem((2, TILE, cols), f32),
-                vmem((2, TILE, cols), i32),
-                vmem((2, FIELDS, HALF, cols), f32),
-                vmem((2, FIELDS, HALF, cols), f32),
+                vmem((2, FIELDS * ITERS, HALF, cols), f32),
+                vmem((2, FIELDS * ITERS, HALF, cols), f32),
                 vmem((2, rows, LANES), f32),
                 vmem((2, rows, LANES), f32),
                 vmem((2, 2, STRIP, LANES), f32),
@@ -691,18 +656,14 @@
                 vmem((2, 1, LANES), f32),
                 vmem((ndev if direct else nlat, 1, LANES), f32),
                 vmem((nlon, 1, LANES), f32),
-                vmem((4, TILE, half), f32),
-                vmem((TILE, half), f32),
-                vmem((TILE, half), f32),
-                vmem((TILE, half), i32),
-                vmem((FIELDS, HALF, half), f32),
+                vmem((FIELDS * ITERS, HALF, half), f32),
                 dma((4,)),
                 dma((nsend,)),
                 dma((nsend,)),
                 dma((npeers,)),
                 dma((npeers,)),
-                dma((10,)),
-                dma((10,)),
+                dma((2,)),
+                dma((2,)),
                 pltpu.SemaphoreType.REGULAR,
             ],
             compiler_params=pltpu.CompilerParams(
@@ -720,9 +681,14 @@
             out_specs=(
                 pl.BlockSpec(memory_space=pl.ANY),
                 pl.BlockSpec(memory_space=pl.ANY),
-                pl.BlockSpec(memory_space=pltpu.SMEM),
+                pl.BlockSpec(memory_space=pl.ANY),
             ),
-            scratch_shapes=[vmem((rows, cols), f32), vmem((rows, cols), f32), dma((2,))],
+            scratch_shapes=[
+                vmem((rows, cols), f32),
+                vmem((rows, cols), f32),
+                pltpu.SMEM((ITERS,), f32),
+                dma((3,)),
+            ],
             compiler_params=pltpu.CompilerParams(vmem_limit_bytes=FINISH_GRANT),
         )(V, U, T)
 

time: 23.2 us -> 22.4 us (0.966)
  Pallas kernels: 22.5 us -> 21.6 us
    pallas_call x1, Pallas kernels: 1.39 us -> 0.88 us  [body(): pl.pallas_call(finish, out_shape=(jax.ShapeDtypeStruct((rows, cols), f32)...]
    pallas_call x1, Pallas kernels: 21.1 us -> 20.7 us  [body(): pl.pallas_call(functools.partial(kernel, nlat, nlon), out_shape=(vmem((IT...]
where the time goes in v3:
time: 22.4 us; the launch traced here: 22.2 us
  Pallas kernels  21.6 us (96%)
  between operations  0.64 us (3%)
    pallas_call x1, Pallas kernels, body(): pl.pallas_call(functools.partial(kernel, nlat, nlon), out_shape=(vmem((IT...  20.7 us
    pallas_call x1, Pallas kernels, body(): pl.pallas_call(finish, out_shape=(jax.ShapeDtypeStruct((rows, cols), f32)...  0.88 us

profile of v3, /device:TPU:0, one launch (start us, length us, event | category | flops | bytes accessed | tf_op | source)
XLA Modules:
  0.0 22.2 jit_solution(804955732338695457)
XLA Ops:
  0.6 20.7 %shard_map.67 = (f32[4,32,1024]{2,1,0:T(8,128)S(1)}, f32[3,32,1024]{2,1,0:T(8,128)S(1)}, f32[8,128]{1,0:T(8,128)S(1)}) custom-call(f32[32,1024]{1,0:T(8,128)} %rhs_in.1, f32[4,32,1024]{2,1,0:T(8,128)} %coef_in.1, f32[32,1024]{1,0:T(8,128)} %extra_in.1, s32[32,1024]{1,0:T(8,128)} %mask_in.1), custom_call_target="tpu_custom_call" | custom-call | tf_op jit(solution)/shard_map/pallas_call | solution.py:633
  21.3 0.9 %shard_map.68 = (f32[32,1024]{1,0:T(8,128)}, f32[32,1024]{1,0:T(8,128)}, f32[3]{0:T(128)}) custom-call(f32[4,32,1024]{2,1,0:T(8,128)S(1)} %get-tuple-element.6.V, f32[3,32,1024]{2,1,0:T(8,128)S(1)} %get-tuple-element.7.U, f32[8,128]{1,0:T(8,128)S(1)} %get-tuple-element.8.T), custom_call_target="tpu_custom_call" | custom-call | tf_op jit(solution)/shard_map/pallas_call | solution.py:673

commit v4 on v3

--- a/solution.py
+++ b/solution.py
@@ -11,7 +11,6 @@
 ITERS = 3
 LOW_EIG = 0.25
 HIGH_EIG = 20.5
-SHIFT = 0.8
 LANES = 128
 TILE = 8
 HALF = 4
@@ -40,8 +39,7 @@
 
 
 def scalars(h, g):
-    c = SHIFT
-    ht = [h[k + 1] + c * h[k] for k in range(len(h) - 1)]
+    ht = [h[k + 1] + h[k] for k in range(len(h) - 1)]
 
     def form(a, t):
         total = None
@@ -73,7 +71,7 @@
         for i in range(len(b)):
             x[i] = x[i] + alpha * b[i]
         tb = [
-            (b[i - 1] if i > 0 else zero) + (c * b[i] if i < len(b) else zero)
+            (b[i - 1] if i > 0 else zero) + (b[i] if i < len(b) else zero)
             for i in range(len(b) + 1)
         ]
         a = [(a[i] if i < len(a) else zero) - alpha * tb[i] for i in range(len(tb))]
@@ -492,7 +490,7 @@
 
             def last_level(i, j, a):
                 at = (ts_of(i), cs_of(j))
-                new = a - SHIFT * VC[at]
+                new = a - VC[at]
                 if it < ITERS - 1:
                     VC[at] = new
                 record(V, it + 1, i, j, new)

time: 22.4 us -> 22.3 us (level)
  no operation moved by 1% of the time
where the time goes in v4:
time: 22.3 us; the launch traced here: 22.2 us
  Pallas kernels  21.5 us (96%)
  between operations  0.64 us (3%)
    pallas_call x1, Pallas kernels, body(): pl.pallas_call(functools.partial(kernel, nlat, nlon), out_shape=(vmem((IT...  20.7 us
    pallas_call x1, Pallas kernels, body(): pl.pallas_call(finish, out_shape=(jax.ShapeDtypeStruct((rows, cols), f32)...  0.87 us

profile of v4, /device:TPU:0, one launch (start us, length us, event | category | flops | bytes accessed | tf_op | source)
XLA Modules:
  0.0 22.2 jit_solution(14550011114878569635)
XLA Ops:
  0.6 20.7 %shard_map.67 = (f32[4,32,1024]{2,1,0:T(8,128)S(1)}, f32[3,32,1024]{2,1,0:T(8,128)S(1)}, f32[8,128]{1,0:T(8,128)S(1)}) custom-call(f32[32,1024]{1,0:T(8,128)} %rhs_in.1, f32[4,32,1024]{2,1,0:T(8,128)} %coef_in.1, f32[32,1024]{1,0:T(8,128)} %extra_in.1, s32[32,1024]{1,0:T(8,128)} %mask_in.1), custom_call_target="tpu_custom_call" | custom-call | tf_op jit(solution)/shard_map/pallas_call | solution.py:631
  21.3 0.9 %shard_map.68 = (f32[32,1024]{1,0:T(8,128)}, f32[32,1024]{1,0:T(8,128)}, f32[3]{0:T(128)}) custom-call(f32[4,32,1024]{2,1,0:T(8,128)S(1)} %get-tuple-element.6.V, f32[3,32,1024]{2,1,0:T(8,128)S(1)} %get-tuple-element.7.U, f32[8,128]{1,0:T(8,128)S(1)} %get-tuple-element.8.T), custom_call_target="tpu_custom_call" | custom-call | tf_op jit(solution)/shard_map/pallas_call | solution.py:671
